TPU v7x, 32 devices: a whole 2x2x4 slice. The times are simulated.
32 devices in a mesh: kv: 16 (over z, y, x), head: 2 (over core).
Axes of the slice: x: 2, y: 2, z: 4, core: 2. Of those that a mesh axis runs over, the one named last changes fastest.
Arguments:
- queries: bfloat16 [8, 256, 128], P('head', 'kv'), may hold values from -384 to 384
- key_cache: bfloat16 [4096, 8, 128, 128], P('kv', 'head'), may hold values from -6 to 6
- value_cache: bfloat16 [4096, 8, 128, 128], P('kv', 'head'), may hold values from -6 to 6
- key_new: bfloat16 [32, 8, 128], P(None, 'head'), may hold values from -6 to 6
- value_new: bfloat16 [32, 8, 128], P(None, 'head'), may hold values from -6 to 6
- lengths: int32 [32], replicated, may hold values from 2 to 16385, as said below
- page_table: int32 [4096], replicated, may hold values from 0 to 4095, each once
Outputs:
- attended: bfloat16 [8, 256, 128], P('head', 'kv')
Inputs may be any that keep to these rules, and one draw needn't show every extreme that they name: The cache holds the first lengths[s] - 1 tokens of sequence s; some sequence has the largest length. `page_table`: every page appears once; page g lies on kv index g // 256.
All inputs are finite; a program needn't handle non-finite values.
Results may differ from a plain program's by a relative error of at most 0.0025.
Values may be sent and summed in bfloat16 or wider, within the bound.
A program may use at most 128 MiB of HBM per device.

v0:
```python
import math
import jax
import jax.numpy as jnp
from jax import lax
from jax.sharding import PartitionSpec as P

LOWEST_SCORE = -1e30


def finish(cache_max, cache_sum, cache_out, query_wide, fresh_key, fresh_value, score_scale):
    new_score = jnp.sum(query_wide * fresh_key.astype(jnp.float32), axis=-1) * score_scale
    highest = jnp.maximum(cache_max, new_score)
    old_part = jnp.exp(cache_max - highest)
    new_part = jnp.exp(new_score - highest)
    numerator = cache_out * old_part[..., None] + new_part[..., None] * fresh_value.astype(
        jnp.float32
    )
    denominator = cache_sum * old_part + new_part
    return (numerator / denominator[..., None]).astype(jnp.bfloat16)


def fold_triples(pieces):
    piece_max, piece_sum, piece_out = pieces
    highest = jnp.max(piece_max, axis=0)
    factor = jnp.exp(piece_max - highest[None])
    return (
        highest,
        jnp.sum(piece_sum * factor, axis=0),
        jnp.sum(piece_out * factor[..., None], axis=0),
    )


def on_device(queries, key_cache, value_cache, key_new, value_new, lengths, page_table):
    all_query = lax.all_gather(queries, "kv", axis=1, tiled=True)
    seq_count = lengths.shape[0]
    page_total = page_table.shape[0]
    pages_here = key_cache.shape[0]
    kv_here = key_cache.shape[1]
    page_len = key_cache.shape[2]
    head_width = key_cache.shape[3]
    rows_all = all_query.shape[1]
    group_size = rows_all // seq_count
    page_slots = page_total // seq_count
    local_rows = queries.shape[1]
    score_scale = 1.0 / math.sqrt(head_width)
    kv_index = lax.axis_index("kv")
    inverse = (
        jnp.zeros((page_total,), jnp.int32)
        .at[page_table]
        .set(jnp.arange(page_total, dtype=jnp.int32))
    )
    local_ids = lax.dynamic_slice_in_dim(inverse, kv_index * pages_here, pages_here)
    page_seq = local_ids // page_slots
    page_slot = local_ids % page_slots
    grouped = all_query.reshape(kv_here, seq_count, group_size, head_width)
    page_query = grouped[:, page_seq]
    scores = (
        jnp.einsum("gpqd,pgtd->pgqt", page_query, key_cache, preferred_element_type=jnp.float32)
        * score_scale
    )
    positions = page_slot[:, None] * page_len + jnp.arange(page_len, dtype=jnp.int32)[None, :]
    in_cache = (positions < (lengths[page_seq] - 1)[:, None])[:, None, None, :]
    masked = jnp.where(in_cache, scores, LOWEST_SCORE)
    page_max = jnp.max(masked, axis=3)
    weights = jnp.where(in_cache, jnp.exp(masked - page_max[..., None]), 0.0)
    page_sum = jnp.sum(weights, axis=3)
    page_out = jnp.einsum(
        "pgqt,pgtd->pgqd",
        weights.astype(jnp.bfloat16),
        value_cache,
        preferred_element_type=jnp.float32,
    )
    member = page_seq[None, :] == jnp.arange(seq_count, dtype=jnp.int32)[:, None]
    seq_best = jnp.max(jnp.where(member[:, :, None, None], page_max[None], LOWEST_SCORE), axis=1)
    factor = jnp.exp(page_max - seq_best[page_seq])
    onehot = member.astype(jnp.float32)
    seq_sum = jnp.einsum("sp,pgq->gsq", onehot, page_sum * factor, precision=lax.Precision.HIGHEST)
    seq_out = jnp.einsum(
        "sp,pgqd->gsqd", onehot, page_out * factor[..., None], precision=lax.Precision.HIGHEST
    )
    seq_max = jnp.transpose(seq_best, (1, 0, 2)).reshape(kv_here, rows_all)
    seq_sum = seq_sum.reshape(kv_here, rows_all)
    seq_out = seq_out.reshape(kv_here, rows_all, head_width)
    cache_max, cache_sum, cache_out = fold_triples(
        (
            lax.all_to_all(seq_max[None], "kv", split_axis=2, concat_axis=0, tiled=True),
            lax.all_to_all(seq_sum[None], "kv", split_axis=2, concat_axis=0, tiled=True),
            lax.all_to_all(seq_out[None], "kv", split_axis=2, concat_axis=0, tiled=True),
        )
    )
    row_seq = (kv_index * local_rows + jnp.arange(local_rows, dtype=jnp.int32)) // group_size
    fresh_key = jnp.transpose(key_new[row_seq], (1, 0, 2))
    fresh_value = jnp.transpose(value_new[row_seq], (1, 0, 2))
    query_wide = queries.astype(jnp.float32)
    return finish(cache_max, cache_sum, cache_out, query_wide, fresh_key, fresh_value, score_scale)


def solution(mesh):
    placed = (
        P("head", "kv", None),
        P("kv", "head", None, None),
        P("kv", "head", None, None),
        P(None, "head", None),
        P(None, "head", None),
        P(),
        P(),
    )
    return jax.shard_map(
        on_device, mesh=mesh, in_specs=placed, out_specs=P("head", "kv", None), check_vma=False
    )
```

profile of v0, /device:TPU:0, one launch (start us, length us, event | category | flops | bytes accessed | tf_op | source)
XLA Modules:
  0.0 175.0 jit_solution(6055094217681499025)
XLA Ops:
  0.0 0.0 copy-start
  0.0 2.1 %fusion.45 = (s32[1]{0:T(128)}, s32[1]{0:T(128)}, s32[1]{0:T(128)}, s32[1]{0:T(128)}, s32[1]{0:T(128)}, /*index=5*/s32[1]{0:T(128)}, s32[1]{0:T(128)}, s32[1]{0:...) fusion(s32[32]{0:T(128)} %param.12), kind=kLoop, calls=%fused_computation.108 | loop fusion | bytes 152 | tf_op jit(solution)/shard_map/gather | solution.py:62
  2.1 1.8 %fusion.46 = (s32[1]{0:T(128)}, s32[1]{0:T(128)}, s32[1]{0:T(128)}, s32[1]{0:T(128)}, s32[1]{0:T(128)}, /*index=5*/s32[1]{0:T(128)}, s32[1]{0:T(128)}, s32[1]{0:...) fusion(s32[32]{0:T(128)} %param.12), kind=kLoop, calls=%fused_computation.109 | loop fusion | bytes 104 | tf_op jit(solution)/shard_map/gather | solution.py:62
  3.9 0.7 compare_select_fusion
  4.7 15.5 %scatter_custom_fusion = s32[4096]{0:T(1024)S(1)} fusion(s32[4096]{0:T(1024)S(1)} %compare_select_fusion, s32[4096]{0:T(1024)S(1)} %iota.23, s32[]{:T(128)} %constant.32.clone.1), kind=kCustom, calls=%fused_computation.48 | custom fusion | bytes 16388 | tf_op jit(solution)/shard_map/scatter | solution.py:50
  20.2 0.1 fusion.35
  20.3 20.1 %fusion.36 = (s32[256]{0:T(256)S(1)}, s32[256]{0:T(256)S(1)}) fusion(s32[]{:T(128)} %bitcast, s32[]{:T(128)} %bitcast.1, s32[]{:T(128)} %bitcast.2, s32[]{:T(128)} %bitcast.3, s32[]{:T(128)} %bitcast.4, s32[]{:T(128)} %bitcast.5, s32[]{:T(128)} %bitcast.6, s32[]{:T(128)} %bitcast.7, s32[]{:T(128)} %bitcast.8, s32[]{:T(128)} %bitcast.9, s32[]{:T(128)} %bitcast.10, ...), kind=kLoop, calls=%fused_computation.100 | loop fusion | flops 20736 | bytes 3204 | tf_op jit(solution)/shard_map/sub | solution.py:62
  40.5 44.0 %all_gather.3 = bf16[4,256,128]{2,1,0:T(8,128)(2,1)S(1)} all-gather(bf16[4,16,128]{2,1,0:T(8,128)(2,1)} %param.7), channel_id=1, replica_groups=mesh['kv'=16,'head'=2] {'kv'}, dimensions={1}, use_global_device_ids=true | all-gather | bytes 278528 | tf_op jit(solution)/shard_map/all_gather | solution.py:34
  84.5 1.3 gather_fusion
  85.9 0.1 add_compare_fusion
  86.0 22.5 %fusion.2 = (f32[256,4,8]{2,1,0:T(4,128)S(1)}, f32[256,4,8,128]{3,2,1,0:T(8,128)}) fusion(pred[256,128]{1,0:T(8,128)(4,1)S(1)} %add_compare_fusion, bf16[256,4,128,128]{3,2,1,0:T(8,128)(2,1)} %param.8, bf16[256,4,8,128]{3,2,1,0:T(8,128)(2,1)S(1)} %gather_fusion), kind=kOutput, calls=%fused_computation.9 | convolution fusion | flops 271572992 | bytes 39911424 | tf_op jit(solution)/shard_map/gpqd,pgtd->pgqt/dot_general | solution.py:58
  108.5 0.2 copy.54
  108.7 0.3 select_reduce_fusion
  109.0 1.0 gather_fusion.1
  110.0 8.4 %fusion.3 = f32[256,4,8]{2,1,0:T(4,128)S(1)} fusion(f32[256,4,8,128]{3,2,1,0:T(8,128)} %get-tuple-element.47, f32[256,4,8]{2,1,0:T(4,128)S(1)} %get-tuple-element.46, pred[256,128]{1,0:T(8,128)(4,1)S(1)} %add_compare_fusion), kind=kLoop, calls=%fused_computation.10 | loop fusion | flops 5234688 | bytes 4292608 | tf_op jit(solution)/shard_map/reduce_sum | solution.py:66
  118.5 0.1 fusion.44
  118.6 0.5 convolution_bitcast_fusion
  119.1 0.8 copy.75
  119.9 3.7 %all-to-all-start.2 = ((f32[1,4,256]{1,0,2:T(1,128)}), f32[1,4,256]{1,0,2:T(1,128)S(1)}, u32[]{:S(2)}, u32[]{:S(2)}) async-start(f32[1,4,256]{1,0,2:T(1,128)} %bitcast.51), calls=%async_computation.2 | async-start | bytes 262144 | tf_op jit(solution)/shard_map/all_to_all | solution.py:87
  123.6 17.7 %broadcast_multiply_fusion = f32[256,4,8,128]{3,2,1,0:T(8,128)} fusion(f32[256,4,8]{2,1,0:T(4,128)S(1)} %bitcast.108, bf16[256,4,128,128]{3,2,1,0:T(8,128)(2,1)} %param.9, f32[256,4,8,128]{3,2,1,0:T(8,128)} %get-tuple-element.47, f32[256,4,8]{2,1,0:T(4,128)S(1)} %get-tuple-element.46, pred[256,128]{1,0:T(8,128)(4,1)S(1)} %add_compare_fusion), kind=kOutput, calls=%fused_computation.15 | convolution fusion | flops 274726912 | bytes 42041344 | tf_op jit(solution)/shard_map/pgqt,pgtd->pgqd/dot_general | solution.py:67
  141.4 0.0 copy-start.1
  141.4 0.0 copy-start.2
  141.4 0.9 copy.74
  142.3 0.0 all-to-all-done.2
  142.3 6.7 %all-to-all-start.1 = ((f32[1,4,256]{1,0,2:T(1,128)}), f32[1,4,256]{1,0,2:T(1,128)S(1)}, u32[]{:S(2)}, u32[]{:S(2)}) async-start(f32[1,4,256]{1,0,2:T(1,128)} %bitcast.42), calls=%async_computation.1 | async-start | bytes 262144 | tf_op jit(solution)/shard_map/all_to_all | solution.py:86
  149.0 5.9 %fusion.16 = f32[4,32,8,128]{3,1,2,0:T(8,128)S(1)} fusion(f32[256,4,8,128]{3,2,1,0:T(8,128)} %broadcast_multiply_fusion, s32[256]{0:T(256)S(1)} %get-tuple-element.13), kind=kOutput, calls=%fused_computation.21 | convolution fusion | flops 402661376 | bytes 4719616 | tf_op jit(solution)/shard_map/sp,pgqd->gsqd/dot_general | solution.py:78
  154.9 0.3 copy.92
  155.2 1.1 copy.57
  156.3 0.5 all-to-all-done.1
  156.8 6.4 %all-to-all-start = ((f32[1,4,256,128]{3,1,0,2:T(4,128)}), f32[1,4,256,128]{3,1,0,2:T(4,128)S(1)}, u32[]{:S(2)}, u32[]{:S(2)}) async-start(f32[1,4,256,128]{3,1,0,2:T(4,128)} %copy.57), calls=%async_computation | async-start | bytes 1048576 | tf_op jit(solution)/shard_map/all_to_all | solution.py:88
  163.3 0.0 copy-done
  163.3 0.6 gather_fusion.2
  163.9 0.0 copy-done.1
  163.9 0.1 fusion.25
  164.0 0.1 copy.63
  164.0 0.0 copy-done.2
  164.1 0.6 gather_fusion.3
  164.6 0.2 copy.70
  164.8 0.2 copy.61
  165.1 0.1 copy.64
  165.2 0.1 copy.66
  165.2 0.1 copy.71
  165.3 8.7 %all-to-all-done = f32[1,4,256,128]{3,1,0,2:T(4,128)S(1)} async-done(((f32[1,4,256,128]{3,1,0,2:T(4,128)}), f32[1,4,256,128]{3,1,0,2:T(4,128)S(1)}, u32[]{:S(2)}, u32[]{:S(2)}) %all-to-all-start) | async-done | bytes 524320 | tf_op jit(solution)/shard_map/all_to_all | solution.py:88
  174.0 0.2 fusion.19
  174.2 0.1 fusion.26
  174.3 0.6 copy.72
  (9 shorter events, 0.1 us)
Async XLA Ops:
  0.0 163.3 %copy-start = (bf16[32,4,128]{2,1,0:T(4,128)(2,1)S(1)}, bf16[32,4,128]{2,1,0:T(4,128)(2,1)}, u32[]{:S(2)}) copy-start(bf16[32,4,128]{2,1,0:T(4,128)(2,1)} %param.10) | copy-start | bytes 98308
  119.9 22.4 %all-to-all-start.2 = ((f32[1,4,256]{1,0,2:T(1,128)}), f32[1,4,256]{1,0,2:T(1,128)S(1)}, u32[]{:S(2)}, u32[]{:S(2)}) async-start(f32[1,4,256]{1,0,2:T(1,128)} %bitcast.51), calls=%async_computation.2 | async-start | bytes 262144 | tf_op jit(solution)/shard_map/all_to_all | solution.py:87
  141.4 22.5 %copy-start.1 = (bf16[4,16,128]{2,1,0:T(8,128)(2,1)S(1)}, bf16[4,16,128]{2,1,0:T(8,128)(2,1)}, u32[]{:S(2)}) copy-start(bf16[4,16,128]{2,1,0:T(8,128)(2,1)} %param.7) | copy-start | bytes 49156
  141.4 22.7 %copy-start.2 = (bf16[32,4,128]{2,1,0:T(4,128)(2,1)S(1)}, bf16[32,4,128]{2,1,0:T(4,128)(2,1)}, u32[]{:S(2)}) copy-start(bf16[32,4,128]{2,1,0:T(4,128)(2,1)} %param.11) | copy-start | bytes 98308
  142.3 14.5 %all-to-all-start.1 = ((f32[1,4,256]{1,0,2:T(1,128)}), f32[1,4,256]{1,0,2:T(1,128)S(1)}, u32[]{:S(2)}, u32[]{:S(2)}) async-start(f32[1,4,256]{1,0,2:T(1,128)} %bitcast.42), calls=%async_computation.1 | async-start | bytes 262144 | tf_op jit(solution)/shard_map/all_to_all | solution.py:86
  156.8 17.2 %all-to-all-start = ((f32[1,4,256,128]{3,1,0,2:T(4,128)}), f32[1,4,256,128]{3,1,0,2:T(4,128)S(1)}, u32[]{:S(2)}, u32[]{:S(2)}) async-start(f32[1,4,256,128]{3,1,0,2:T(4,128)} %copy.57), calls=%async_computation | async-start | bytes 1048576 | tf_op jit(solution)/shard_map/all_to_all | solution.py:88
where the time goes:
time: 176 us; the launch traced here: 175 us
  matrix products  46.7 us (27%)
  blocking collectives  44 us (25%)
  other arithmetic  30.5 us (17%)
  local copies, waits for them, and re-layouts  27.6 us (16%)
  starting transfers between devices  16.8 us (10%)
  waiting for transfers between devices  9.15 us (5%)
    all_gather x1, blocking collectives, on_device(): all_query = lax.all_gather(queries, 'kv', axis=1, tiled=True)  44 us
    dot_general x1, matrix products, on_device(): jnp.einsum('gpqd,pgtd->pgqt', page_query, key_cache, preferred_element_ty...  22.5 us
    sub x1, other arithmetic, on_device(): in_cache = (positions < (lengths[page_seq] - 1)[:, None])[:, None, None, :]  20.1 us
    dot_general x1, matrix products, on_device(): jnp.einsum('pgqt,pgtd->pgqd', weights.astype(jnp.bfloat16), value_cache,...  17.7 us
    scatter x1, local copies, waits for them, and re-layouts, on_device(): inverse = jnp.zeros((page_total,), jnp.int32).at[page_table].set(jnp.aran...  15.5 us
    all_to_all x1, waiting for transfers between devices, on_device(): lax.all_to_all(seq_out[None], 'kv', split_axis=2, concat_axis=0, tiled=True)  8.68 us
    reduce_sum x1, other arithmetic, on_device(): page_sum = jnp.sum(weights, axis=3)  8.45 us
    all_to_all x1, starting transfers between devices, on_device(): lax.all_to_all(seq_max[None], 'kv', split_axis=2, concat_axis=0, tiled=True)  6.69 us
  transfers between devices with their start and end apart: 3, of which 2 were waited for; matrix products, arithmetic and copies ran while one was open for 16% of the time, Pallas kernels for 0%

commit v1 on v0

--- a/solution.py
+++ b/solution.py
@@ -81,11 +81,20 @@
     seq_max = jnp.transpose(seq_best, (1, 0, 2)).reshape(kv_here, rows_all)
     seq_sum = seq_sum.reshape(kv_here, rows_all)
     seq_out = seq_out.reshape(kv_here, rows_all, head_width)
+    _state_numbers = lambda frame, named_axis: jnp.concatenate(
+        lax.all_to_all(
+            jnp.stack(jnp.split(frame, lax.psum(1, axis_name=named_axis), 2), 0),
+            axis_name=named_axis,
+            split_axis=0,
+            concat_axis=0,
+        ),
+        0,
+    )
     cache_max, cache_sum, cache_out = fold_triples(
         (
             lax.all_to_all(seq_max[None], "kv", split_axis=2, concat_axis=0, tiled=True),
             lax.all_to_all(seq_sum[None], "kv", split_axis=2, concat_axis=0, tiled=True),
-            lax.all_to_all(seq_out[None], "kv", split_axis=2, concat_axis=0, tiled=True),
+            _state_numbers(seq_out[None], "kv"),
         )
     )
     row_seq = (kv_index * local_rows + jnp.arange(local_rows, dtype=jnp.int32)) // group_size

time: 176 us -> 188 us (1.068)
  local copies, waits for them, and re-layouts: 27.6 us -> 36.1 us
  waiting for transfers between devices: 9.15 us -> 15.9 us
  starting transfers between devices: 16.8 us -> 14 us
    unnamed x6 -> x21, local copies, waits for them, and re-layouts: 0.01 us -> 9.08 us
    all_to_all x1, waiting for transfers between devices: 0.47 us -> 7.3 us  [on_device(): lax.all_to_all(seq_max[None], 'kv', split_axis=2, concat_axis=0, tiled=True)]
    all_to_all x1, starting transfers between devices: 6.44 us -> 3.57 us  [on_device(): lax.all_to_all(jnp.stack(jnp.split(frame, lax.psum(1, axis_name=named_axi...]
  transfers between devices with their start and end apart: 3 -> 3, of which waited for: 2 -> 2; matrix products, arithmetic and copies ran while one was open for 16% -> 20% of each run, Pallas kernels for 0% -> 0%
where the time goes in v1:
time: 188 us; the launch traced here: 187 us
  matrix products  46.8 us (25%)
  blocking collectives  44 us (23%)
  local copies, waits for them, and re-layouts  36.1 us (19%)
  other arithmetic  30.5 us (16%)
  waiting for transfers between devices  15.9 us (8%)
  starting transfers between devices  14 us (7%)
    all_gather x1, blocking collectives, on_device(): all_query = lax.all_gather(queries, 'kv', axis=1, tiled=True)  44 us
    dot_general x1, matrix products, on_device(): jnp.einsum('gpqd,pgtd->pgqt', page_query, key_cache, preferred_element_ty...  22.5 us
    sub x1, other arithmetic, on_device(): in_cache = (positions < (lengths[page_seq] - 1)[:, None])[:, None, None, :]  20.1 us
    dot_general x1, matrix products, on_device(): jnp.einsum('pgqt,pgtd->pgqd', weights.astype(jnp.bfloat16), value_cache,...  17.8 us
    scatter x1, local copies, waits for them, and re-layouts, on_device(): inverse = jnp.zeros((page_total,), jnp.int32).at[page_table].set(jnp.aran...  15.5 us
    unnamed x21, local copies, waits for them, and re-layouts  9.08 us
    all_to_all x1, waiting for transfers between devices, on_device(): lax.all_to_all(jnp.stack(jnp.split(frame, lax.psum(1, axis_name=named_axi...  8.62 us
    reduce_sum x1, other arithmetic, on_device(): page_sum = jnp.sum(weights, axis=3)  8.45 us
  transfers between devices with their start and end apart: 3, of which 2 were waited for; matrix products, arithmetic and copies ran while one was open for 20% of the time, Pallas kernels for 0%

profile of v1, /device:TPU:0, one launch (start us, length us, event | category | flops | bytes accessed | tf_op | source)
XLA Modules:
  0.0 187.5 jit_solution(9169428817913725714)
XLA Ops:
  0.0 0.0 copy-start
  0.0 2.1 %fusion.61 = (s32[1]{0:T(128)}, s32[1]{0:T(128)}, s32[1]{0:T(128)}, s32[1]{0:T(128)}, s32[1]{0:T(128)}, /*index=5*/s32[1]{0:T(128)}, s32[1]{0:T(128)}, s32[1]{0:...) fusion(s32[32]{0:T(128)} %param.12), kind=kLoop, calls=%fused_computation.140 | loop fusion | bytes 152 | tf_op jit(solution)/shard_map/gather | solution.py:62
  2.1 1.8 fusion.62
  3.9 0.7 compare_select_fusion
  4.7 15.5 %scatter_custom_fusion = s32[4096]{0:T(1024)S(1)} fusion(s32[4096]{0:T(1024)S(1)} %compare_select_fusion, s32[4096]{0:T(1024)S(1)} %iota.23, s32[]{:T(128)} %constant.32.clone.1), kind=kCustom, calls=%fused_computation.80 | custom fusion | bytes 16388 | tf_op jit(solution)/shard_map/scatter | solution.py:50
  20.2 0.1 fusion.51
  20.3 20.1 %fusion.52 = (s32[256]{0:T(256)S(1)}, s32[256]{0:T(256)S(1)}) fusion(s32[]{:T(128)} %bitcast, s32[]{:T(128)} %bitcast.1, s32[]{:T(128)} %bitcast.2, s32[]{:T(128)} %bitcast.3, s32[]{:T(128)} %bitcast.4, s32[]{:T(128)} %bitcast.5, s32[]{:T(128)} %bitcast.6, s32[]{:T(128)} %bitcast.7, s32[]{:T(128)} %bitcast.8, s32[]{:T(128)} %bitcast.9, s32[]{:T(128)} %bitcast.10, ...), kind=kLoop, calls=%fused_computation.132 | loop fusion | flops 20736 | bytes 3204 | tf_op jit(solution)/shard_map/sub | solution.py:62
  40.5 44.0 %all_gather.3 = bf16[4,256,128]{2,1,0:T(8,128)(2,1)S(1)} all-gather(bf16[4,16,128]{2,1,0:T(8,128)(2,1)} %param.7), channel_id=1, replica_groups=mesh['kv'=16,'head'=2] {'kv'}, dimensions={1}, use_global_device_ids=true | all-gather | bytes 278528 | tf_op jit(solution)/shard_map/all_gather | solution.py:34
  84.5 1.3 gather_fusion
  85.9 0.1 add_compare_fusion
  86.0 22.5 %fusion.2 = (f32[256,4,8]{2,1,0:T(4,128)S(1)}, f32[256,4,8,128]{3,2,1,0:T(8,128)}) fusion(pred[256,128]{1,0:T(8,128)(4,1)S(1)} %add_compare_fusion, bf16[256,4,128,128]{3,2,1,0:T(8,128)(2,1)} %param.8, bf16[256,4,8,128]{3,2,1,0:T(8,128)(2,1)S(1)} %gather_fusion), kind=kOutput, calls=%fused_computation.9 | convolution fusion | flops 271572992 | bytes 39911424 | tf_op jit(solution)/shard_map/gpqd,pgtd->pgqt/dot_general | solution.py:58
  108.5 0.2 copy.53
  108.7 0.3 select_reduce_fusion
  109.0 1.0 gather_fusion.1
  110.0 8.4 %fusion.3 = f32[256,4,8]{2,1,0:T(4,128)S(1)} fusion(f32[256,4,8,128]{3,2,1,0:T(8,128)} %get-tuple-element.47, f32[256,4,8]{2,1,0:T(4,128)S(1)} %get-tuple-element.46, pred[256,128]{1,0:T(8,128)(4,1)S(1)} %add_compare_fusion), kind=kLoop, calls=%fused_computation.10 | loop fusion | flops 5234688 | bytes 4292608 | tf_op jit(solution)/shard_map/reduce_sum | solution.py:66
  118.5 0.1 fusion.60
  118.6 0.5 convolution_bitcast_fusion
  119.1 0.8 copy.74
  119.9 3.7 %all-to-all-start.2 = ((f32[1,4,256]{1,0,2:T(1,128)}), f32[1,4,256]{1,0,2:T(1,128)S(1)}, u32[]{:S(2)}, u32[]{:S(2)}) async-start(f32[1,4,256]{1,0,2:T(1,128)} %bitcast.65), calls=%async_computation.2 | async-start | bytes 262144 | tf_op jit(solution)/shard_map/all_to_all | solution.py:96
  123.6 17.8 %broadcast_multiply_fusion = f32[256,4,8,128]{3,2,1,0:T(8,128)} fusion(f32[256,4,8]{2,1,0:T(4,128)S(1)} %bitcast.183, bf16[256,4,128,128]{3,2,1,0:T(8,128)(2,1)} %param.9, f32[256,4,8,128]{3,2,1,0:T(8,128)} %get-tuple-element.47, f32[256,4,8]{2,1,0:T(4,128)S(1)} %get-tuple-element.46, pred[256,128]{1,0:T(8,128)(4,1)S(1)} %add_compare_fusion), kind=kOutput, calls=%fused_computation.15 | convolution fusion | flops 274726912 | bytes 42041344 | tf_op jit(solution)/shard_map/pgqt,pgtd->pgqd/dot_general | solution.py:67
  141.4 0.0 copy-start.1
  141.4 0.0 copy-start.2
  141.4 5.9 %fusion.16 = f32[4,32,8,128]{3,1,2,0:T(8,128)S(1)} fusion(f32[256,4,8,128]{3,2,1,0:T(8,128)} %broadcast_multiply_fusion, s32[256]{0:T(256)S(1)} %get-tuple-element.13), kind=kOutput, calls=%fused_computation.21 | convolution fusion | flops 402661376 | bytes 4719616 | tf_op jit(solution)/shard_map/sp,pgqd->gsqd/dot_general | solution.py:78
  147.3 0.3 copy.91
  147.6 0.6 fusion.36
  148.2 0.6 fusion.35
  148.9 0.6 fusion.34
  149.5 0.6 fusion.33
  150.1 0.6 fusion.32
  150.7 0.6 fusion.31
  151.3 0.6 fusion.30
  151.9 0.6 fusion.29
  152.5 0.6 fusion.28
  153.1 0.6 fusion.27
  153.7 0.6 fusion.26
  154.3 0.6 fusion.25
  154.9 0.6 fusion.24
  155.5 0.6 fusion.23
  156.1 0.6 fusion.22
  156.7 0.9 copy.72
  157.6 0.0 all-to-all-done.2
  157.6 6.7 %all-to-all-start.1 = ((f32[1,4,256]{1,0,2:T(1,128)}), f32[1,4,256]{1,0,2:T(1,128)S(1)}, u32[]{:S(2)}, u32[]{:S(2)}) async-start(f32[1,4,256]{1,0,2:T(1,128)} %bitcast.56), calls=%async_computation.1 | async-start | bytes 262144 | tf_op jit(solution)/shard_map/all_to_all | solution.py:95
  164.3 0.6 fusion.21
  164.9 7.3 %all-to-all-done.1 = f32[1,4,256]{1,0,2:T(1,128)S(1)} async-done(((f32[1,4,256]{1,0,2:T(1,128)}), f32[1,4,256]{1,0,2:T(1,128)S(1)}, u32[]{:S(2)}, u32[]{:S(2)}) %all-to-all-start.1) | async-done | bytes 4128 | tf_op jit(solution)/shard_map/all_to_all | solution.py:95
  172.2 3.6 %all-to-all-start = ((f32[16,1,4,16,128]{4,3,2,1,0:T(8,128)}), f32[16,1,4,16,128]{4,3,2,1,0:T(8,128)S(1)}, u32[]{:S(2)}, u32[]{:S(2)}) async-start(f32[16,1,4,16,128]{4,3,2,1,0:T(8,128)} %fusion.21), calls=%async_computation | async-start | bytes 1048576 | tf_op jit(solution)/shard_map/all_to_all | solution.py:85
  175.9 0.0 copy-done
  175.9 0.6 gather_fusion.2
  176.5 0.0 copy-done.1
  176.5 0.1 fusion.41
  176.6 0.1 copy.61
  176.6 0.0 copy-done.2
  176.6 0.6 gather_fusion.3
  177.2 0.2 copy.75
  177.4 0.2 copy.73
  177.7 0.1 copy.62
  177.8 0.1 copy.64
  177.8 0.1 copy.69
  177.9 8.6 %all-to-all-done = f32[16,1,4,16,128]{4,3,2,1,0:T(8,128)S(1)} async-done(((f32[16,1,4,16,128]{4,3,2,1,0:T(8,128)}), f32[16,1,4,16,128]{4,3,2,1,0:T(8,128)S(1)}, u32[]{:S(2)}, u32[]{:S(2)}) %all-to-all-start) | async-done | bytes 524320 | tf_op jit(solution)/shard_map/all_to_all | solution.py:85
  186.6 0.2 fusion.19
  186.8 0.1 fusion.42
  186.9 0.6 copy.70
  (10 shorter events, 0.1 us)
Async XLA Ops:
  0.0 175.9 %copy-start = (bf16[32,4,128]{2,1,0:T(4,128)(2,1)S(1)}, bf16[32,4,128]{2,1,0:T(4,128)(2,1)}, u32[]{:S(2)}) copy-start(bf16[32,4,128]{2,1,0:T(4,128)(2,1)} %param.10) | copy-start | bytes 98308
  119.9 37.7 %all-to-all-start.2 = ((f32[1,4,256]{1,0,2:T(1,128)}), f32[1,4,256]{1,0,2:T(1,128)S(1)}, u32[]{:S(2)}, u32[]{:S(2)}) async-start(f32[1,4,256]{1,0,2:T(1,128)} %bitcast.65), calls=%async_computation.2 | async-start | bytes 262144 | tf_op jit(solution)/shard_map/all_to_all | solution.py:96
  141.4 35.0 %copy-start.1 = (bf16[4,16,128]{2,1,0:T(8,128)(2,1)S(1)}, bf16[4,16,128]{2,1,0:T(8,128)(2,1)}, u32[]{:S(2)}) copy-start(bf16[4,16,128]{2,1,0:T(8,128)(2,1)} %param.7) | copy-start | bytes 49156
  141.4 35.2 %copy-start.2 = (bf16[32,4,128]{2,1,0:T(4,128)(2,1)S(1)}, bf16[32,4,128]{2,1,0:T(4,128)(2,1)}, u32[]{:S(2)}) copy-start(bf16[32,4,128]{2,1,0:T(4,128)(2,1)} %param.11) | copy-start | bytes 98308
  157.6 14.6 %all-to-all-start.1 = ((f32[1,4,256]{1,0,2:T(1,128)}), f32[1,4,256]{1,0,2:T(1,128)S(1)}, u32[]{:S(2)}, u32[]{:S(2)}) async-start(f32[1,4,256]{1,0,2:T(1,128)} %bitcast.56), calls=%async_computation.1 | async-start | bytes 262144 | tf_op jit(solution)/shard_map/all_to_all | solution.py:95
  172.2 14.3 %all-to-all-start = ((f32[16,1,4,16,128]{4,3,2,1,0:T(8,128)}), f32[16,1,4,16,128]{4,3,2,1,0:T(8,128)S(1)}, u32[]{:S(2)}, u32[]{:S(2)}) async-start(f32[16,1,4,16,128]{4,3,2,1,0:T(8,128)} %fusion.21), calls=%async_computation | async-start | bytes 1048576 | tf_op jit(solution)/shard_map/all_to_all | solution.py:85
